TPU v7x, 32 devices: a whole 2x2x4 slice. The times are simulated.
32 devices in a mesh: gx: 4 (over z), gy: 4 (over y, x), gz: 2 (over core).
Axes of the slice: x: 2, y: 2, z: 4, core: 2. Of those that a mesh axis runs over, the one named last changes fastest.
Arguments:
- positions: float32 [3, 64, 64, 512], P(None, 'gx', 'gy', 'gz'), may hold values from -6 to 6
- pair_node: int32 [4, 4, 2, 32, 256], P('gx', 'gy', 'gz'), may hold values from 0 to 255
- pair_line: int32 [4, 4, 2, 32], P('gx', 'gy', 'gz'), may hold values from 0 to 255
- pair_far: int32 [4, 4, 2, 32, 256], P('gx', 'gy', 'gz'), may hold values from 0 to 261, as said below
- far_line: int32 [4, 4, 2, 32], P('gx', 'gy', 'gz'), may hold values from 0 to 483, as said below
- pair_geom: float32 [4, 4, 2, 32, 4, 256], P('gx', 'gy', 'gz'), may hold values from -4 to 4
- live_blocks: int32 [4, 4, 2], P('gx', 'gy', 'gz'), may hold values from 8 to 32, as said below
Outputs:
- corrected: float32 [3, 64, 64, 512], P(None, 'gx', 'gy', 'gz')
- sweep_history: float32 [2, 5], replicated
Inputs may be any that keep to these rules, and one draw needn't show every extreme that they name: `pair_far`: together with far_line: at most one of the three coordinates of node b lies outside the owner block's own nodes; node b lies inside the whole grid; in slots below 16 node b is one of the owner block's own nodes. `far_line`: together with pair_far, as stated there. `live_blocks`: some owner block has all 32 slots live.
All inputs are finite; a program needn't handle non-finite values.
Results may differ from a plain program's by a relative error of at most 0.0001.
Values sent between devices are 32-bit elements; how exact they have to be, the bound alone decides.
A program may use at most 64 MiB of HBM per device.

v0:
```python
import math
import jax
import jax.numpy as jnp
from jax import lax
from jax.sharding import PartitionSpec as P

RIM = 3
SWEEPS = 5
relax_factor = 0.9
highest = lax.Precision.HIGHEST


def extended(cells, sides, width):
    for axis, dim in sides:
        count = lax.axis_size(axis)
        ends = count - 1
        head = lax.slice_in_dim(cells, 0, width, axis=dim)
        tail = lax.slice_in_dim(cells, cells.shape[dim] - width, cells.shape[dim], axis=dim)
        cells = jnp.concatenate(
            [
                lax.ppermute(tail, axis, [(i, (i + 1) % count) for i in range(ends)]),
                cells,
                lax.ppermute(head, axis, [((i + 1) % count, i) for i in range(ends)]),
            ],
            axis=dim,
        )
    return cells


def node_sums(contribs, within, line_index, line_length, count_lines):
    blocks = contribs.shape[0]
    group_size = math.gcd(16, blocks)
    row_count = contribs.shape[1]
    columns = lax.broadcasted_iota(jnp.int32, (1, 1, line_length), 2)
    line_ids = lax.broadcasted_iota(jnp.int32, (1, count_lines), 1)

    def node_add_group(turn_idx, running):
        first_block = turn_idx * group_size
        term_part = lax.dynamic_slice_in_dim(contribs, first_block, group_size, 0)
        node_part = lax.dynamic_slice_in_dim(within, first_block, group_size, 0)
        line_part = lax.dynamic_slice_in_dim(line_index, first_block, group_size, 0)
        one_hot = (node_part[:, :, None] == columns).astype(jnp.float32)
        window = jnp.einsum("bcp,bpn->bcn", term_part, one_hot, precision=highest)
        line_hot = (line_part[:, None] == line_ids).astype(jnp.float32)
        return running + jnp.einsum("bl,bcn->cln", line_hot, window, precision=highest)

    initial = jnp.zeros((row_count, count_lines, line_length), jnp.float32)
    return lax.fori_loop(0, blocks // group_size, node_add_group, initial)


def select_lines(line_hot, field_lines):
    return jnp.einsum("bl,cln->bcn", line_hot, field_lines, precision=highest)


def sweep_terms(
    near_lines, far_lines, within, far_pos, line_index, geometry, live_mask, count_lines
):
    blocks = within.shape[0]
    group_size = math.gcd(16, blocks)
    near_cols = lax.broadcasted_iota(jnp.int32, (1, 1, near_lines.shape[2]), 2)
    far_cols = lax.broadcasted_iota(jnp.int32, (1, 1, far_lines.shape[2]), 2)
    line_ids = lax.broadcasted_iota(jnp.int32, (1, count_lines), 1)

    def sweep_add_group(turn_idx, carry):
        running, energy_sum = carry
        near_hot = (within[:, :, None] == near_cols).astype(jnp.float32)
        far_hot = (far_pos[:, :, None] == far_cols).astype(jnp.float32)
        near_vals = jnp.einsum("bcn,bpn->bcp", near_lines, near_hot, precision=highest)
        far_vals = jnp.einsum("bcn,bpn->bcp", far_lines, far_hot, precision=highest)
        differ = near_vals - far_vals
        gap_value = (
            geometry[:, 0, :] * differ[:, 0, :]
            + geometry[:, 1, :] * differ[:, 1, :]
            + geometry[:, 2, :] * differ[:, 2, :]
            - geometry[:, 3, :]
        )
        depth_value = jnp.where(live_mask, jnp.maximum(-gap_value, 0.0), 0.0)
        contribs = depth_value[:, None, :] * geometry[:, 0:3, :]
        window = jnp.einsum("bcp,bpn->bcn", contribs, near_hot, precision=highest)
        line_hot = (line_index[:, None] == line_ids).astype(jnp.float32)
        running = running + jnp.einsum("bl,bcn->cln", line_hot, window, precision=highest)
        return (running, energy_sum + jnp.sum(depth_value * depth_value))

    initial = (
        jnp.zeros((3, count_lines, near_lines.shape[2]), jnp.float32),
        jnp.zeros((), jnp.float32),
    )
    return lax.fori_loop(0, blocks // group_size, sweep_add_group, initial)


def local(positions, pair_node, pair_line, pair_far, far_line, pair_geom, live_blocks):
    within = pair_node[0, 0, 0]
    line_index = pair_line[0, 0, 0]
    far_pos = pair_far[0, 0, 0]
    far_index = far_line[0, 0, 0]
    geometry = pair_geom[0, 0, 0]
    live_count = live_blocks[0, 0, 0]
    size_x = positions.shape[1]
    size_y = positions.shape[2]
    size_z = positions.shape[3]
    blocks = within.shape[0]
    pair_count = within.shape[1]
    inner_count = blocks // 2
    count_lines = size_x * size_y
    ext_lines = (size_x + 2 * RIM) * (size_y + 2 * RIM)
    ext_z = size_z + 2 * RIM
    devices = lax.axis_size("gx") * lax.axis_size("gy") * lax.axis_size("gz")
    slot_count = blocks * pair_count
    live_mask = lax.broadcasted_iota(jnp.int32, (blocks, 1), 0) < live_count
    near_hot = (line_index[:, None] == lax.broadcasted_iota(jnp.int32, (1, count_lines), 1)).astype(
        jnp.float32
    )
    far_hot = (far_index[:, None] == lax.broadcasted_iota(jnp.int32, (1, ext_lines), 1)).astype(
        jnp.float32
    )
    live_ones = jnp.broadcast_to(
        jnp.where(live_mask, 1.0, 0.0).astype(jnp.float32), (blocks, pair_count)
    )
    counts = node_sums(live_ones[:, None, :], within, line_index, size_z, count_lines).reshape(
        size_x, size_y, size_z
    )
    widths = ((0, 0), (RIM, RIM), (RIM, RIM), (RIM, RIM))
    padded = extended(positions, (("gx", 1), ("gy", 2), ("gz", 3)), RIM)
    current = positions
    energies = []
    residuals = []
    for sweep_idx in range(SWEEPS):
        near_lines = select_lines(near_hot, current.reshape(3, count_lines, size_z))
        local_pad = jnp.pad(current, widths).reshape(3, ext_lines, ext_z)
        inner_far = select_lines(far_hot[:inner_count], local_pad)
        inner_total, inner_energy = sweep_terms(
            near_lines[:inner_count],
            inner_far,
            within[:inner_count],
            far_pos[:inner_count],
            line_index[:inner_count],
            geometry[:inner_count],
            live_mask[:inner_count],
            count_lines,
        )
        outer_far = select_lines(far_hot[inner_count:], padded.reshape(3, ext_lines, ext_z))
        outer_total, outer_energy = sweep_terms(
            near_lines[inner_count:],
            outer_far,
            within[inner_count:],
            far_pos[inner_count:],
            line_index[inner_count:],
            geometry[inner_count:],
            live_mask[inner_count:],
            count_lines,
        )
        node_total = inner_total + outer_total
        energy_local = inner_energy + outer_energy
        total_energy = lax.psum(energy_local, ("gx", "gy", "gz"))
        scale_factor = 1.0 / (1.0 + total_energy / (slot_count * devices))
        correction = (
            relax_factor
            * scale_factor
            * node_total.reshape(3, size_x, size_y, size_z)
            / (1.0 + counts)
        )
        current = current + correction
        residual_local = jnp.sum(correction * correction)
        residuals.append(lax.psum(residual_local, ("gx", "gy", "gz")))
        energies.append(total_energy)
        if sweep_idx + 1 < SWEEPS:
            padded = extended(current, (("gx", 1), ("gy", 2), ("gz", 3)), RIM)
    history = jnp.stack(
        [
            jnp.sqrt(1.0 + jnp.stack(energies) / slot_count),
            jnp.sqrt(1.0 + jnp.stack(residuals) / (size_x * size_y * size_z)),
        ]
    )
    return (current, history)


def solution(mesh):
    return jax.shard_map(
        local,
        mesh=mesh,
        in_specs=(
            P(None, "gx", "gy", "gz"),
            P("gx", "gy", "gz", None, None),
            P("gx", "gy", "gz", None),
            P("gx", "gy", "gz", None, None),
            P("gx", "gy", "gz", None),
            P("gx", "gy", "gz", None, None, None),
            P("gx", "gy", "gz"),
        ),
        out_specs=(P(None, "gx", "gy", "gz"), P()),
        check_vma=False,
    )
```

profile of v0, /device:TPU:0, one launch (start us, length us, event | category | flops | bytes accessed | tf_op | source)
XLA Modules:
  0.0 585.4 jit_solution(6506297491511349636)
XLA Ops:
  3.7 5.6 collective-permute-start
  11.4 2.0 pad.16
  13.4 3.0 reshape.413
  17.5 2.5 fusion.244
  21.6 2.1 fusion.78
  26.3 4.3 while.9
  33.4 4.6 collective-permute-start.2
  38.0 2.8 fusion.32
  46.5 4.1 collective-permute-start.4
  54.9 2.4 pad_maximum_fusion
  59.5 2.6 fusion.249
  66.3 44.0 %psum.70 = f32[]{:T(128)} all-reduce(f32[]{:T(128)S(6)} %add.349), channel_id=1, replica_groups=mesh['gx'=4,'gy'=4,'gz'=2] {'gx','gy','gz'}, use_global_device_ids=true, to_apply=%region_2.3 | all-reduce | flops 1 | bytes 8 | tf_op jit(solution)/shard_map/psum | solution.py:154
  114.8 4.6 collective-permute-start.6
  123.5 4.8 collective-permute-start.8
  128.3 2.1 fusion.40
  138.4 3.8 collective-permute-start.10
  142.2 3.6 fusion.30
  147.7 5.1 pad_maximum_fusion.1
  152.8 3.0 reshape.416
  155.8 2.5 fusion.243
  162.3 3.0 reshape.417
  165.3 2.5 fusion.248
  171.9 43.0 %psum.71 = f32[]{:T(128)} all-reduce(f32[]{:T(128)S(6)} %add.359), channel_id=1, replica_groups=mesh['gx'=4,'gy'=4,'gz'=2] {'gx','gy','gz'}, use_global_device_ids=true, to_apply=%region_7.8 | all-reduce | flops 1 | bytes 8 | tf_op jit(solution)/shard_map/psum | solution.py:154
  219.3 5.0 collective-permute-start.12
  228.0 4.8 collective-permute-start.14
  232.9 2.8 fusion.38
  242.1 3.0 collective-permute-start.16
  245.2 3.6 fusion.28
  251.6 5.0 pad_maximum_fusion.2
  256.5 3.0 reshape.419
  259.5 2.5 fusion.242
  262.0 2.3 fusion.20
  265.1 2.2 fusion.37
  269.0 2.5 fusion.247
  271.5 2.3 fusion.15
  276.5 44.2 %psum.72 = f32[]{:T(128)} all-reduce(f32[]{:T(128)S(6)} %add.367), channel_id=1, replica_groups=mesh['gx'=4,'gy'=4,'gz'=2] {'gx','gy','gz'}, use_global_device_ids=true, to_apply=%region_10.11 | all-reduce | flops 1 | bytes 8 | tf_op jit(solution)/shard_map/psum | solution.py:154
  325.2 4.7 collective-permute-start.18
  333.9 4.8 collective-permute-start.20
  338.7 2.1 fusion.36
  348.6 3.7 collective-permute-start.22
  352.3 3.6 fusion.26
  357.8 5.1 pad_maximum_fusion.3
  362.9 3.0 reshape.422
  365.9 2.5 fusion.241
  372.4 3.0 reshape.423
  375.5 2.5 fusion.246
  382.0 43.2 %psum.73 = f32[]{:T(128)} all-reduce(f32[]{:T(128)S(6)} %add.375), channel_id=1, replica_groups=mesh['gx'=4,'gy'=4,'gz'=2] {'gx','gy','gz'}, use_global_device_ids=true, to_apply=%region_13.14 | all-reduce | flops 1 | bytes 8 | tf_op jit(solution)/shard_map/psum | solution.py:154
  429.6 4.8 collective-permute-start.24
  438.3 4.8 collective-permute-start.26
  443.2 2.8 fusion.34
  452.4 3.0 collective-permute-start.28
  455.4 3.6 fusion.24
  461.8 5.0 pad_maximum_fusion.4
  466.8 3.0 reshape.425
  469.8 2.5 fusion.240
  472.3 2.3 fusion.18
  480.0 2.6 fusion.245
  482.7 2.3 fusion.13
  487.8 2.3 fusion.23
  490.1 44.1 %psum.74 = f32[]{:T(128)} all-reduce(f32[]{:T(128)S(6)} %add.383), channel_id=1, replica_groups=mesh['gx'=4,'gy'=4,'gz'=2] {'gx','gy','gz'}, use_global_device_ids=true, to_apply=%region_16.17 | all-reduce | flops 1 | bytes 8 | tf_op jit(solution)/shard_map/psum | solution.py:154
  534.9 3.1 fusion.88
  539.1 39.2 %all-reduce.5 = (f32[1,1]{1,0:T(1,128)}, f32[1,1]{1,0:T(1,128)}, f32[1,1]{1,0:T(1,128)}, f32[1,1]{1,0:T(1,128)}, f32[1,1]{1,0:T(1,128)}) all-reduce(f32[1,1]{1,0:T(1,128)} %bitcast.57, f32[1,1]{1,0:T(1,128)} %bitcast.58, f32[1,1]{1,0:T(1,128)} %bitcast.59, ...), channel_id=1, replica_groups=mesh['gx'=4,'gy'=4,'gz'=2] {'gx','gy','gz'}, use_global_device_ids=true, to_apply=%region_18.19 | all-reduce | flops 5 | bytes 40 | tf_op jit(solution)/shard_map/psum | solution.py:164
  578.3 3.1 stack.52
  581.4 3.1 stack.46
  (362 shorter events, 126.4 us)
Async XLA Ops:
  0.6 10.8 %copy-start = (f32[3,16,16,256]{3,2,1,0:T(8,128)S(1)}, f32[3,16,16,256]{3,2,1,0:T(8,128)}, u32[]{:S(2)}) copy-start(f32[3,16,16,256]{3,2,1,0:T(8,128)} %param.9) | copy-start | bytes 2359300
  0.6 9.4 %copy-start.34 = (f32[1,1,1,32,4,256]{5,4,3,2,1,0:T(4,128)S(1)}, f32[1,1,1,32,4,256]{5,4,3,2,1,0:T(4,128)}, u32[]{:S(2)}) copy-start(f32[1,1,1,32,4,256]{5,4,3,2,1,0:T(4,128)} %param.14) | copy-start | bytes 393220
  0.6 10.2 %copy-start.44 = (s32[1,1,1,32,256]{4,3,2,1,0:T(8,128)S(1)}, s32[1,1,1,32,256]{4,3,2,1,0:T(8,128)}, u32[]{:S(2)}) copy-start(s32[1,1,1,32,256]{4,3,2,1,0:T(8,128)} %param.12) | copy-start | bytes 98308
  2.4 29.6 %collective-permute-start.1 = (f32[3,3,16,256]{3,1,2,0:T(4,128)S(1)}, f32[3,3,16,256]{3,1,2,0:T(4,128)S(1)}, u32[]{:S(2)}, u32[]{:S(2)}) collective-permute-start(f32[3,3,16,256]{3,1,2,0:T(4,128)S(1)} %get-tuple-element.616), channel_id=1, source_target_pairs={{8,0},{16,8},{24,16},{9,1},{17,9},{25,17},{10,2},{18,10},{26,18},{... | collective-permute-start | bytes 442376 | tf_op jit(solution)/shard_map/ppermute | solution.py:23
  3.7 28.3 %collective-permute-start = (f32[3,3,16,256]{3,1,2,0:T(4,128)S(1)}, f32[3,3,16,256]{3,1,2,0:T(4,128)S(1)}, u32[]{:S(2)}, u32[]{:S(2)}) collective-permute-start(f32[3,3,16,256]{3,1,2,0:T(4,128)S(1)} %get-tuple-element.615), channel_id=1, source_target_pairs={{0,8},{8,16},{16,24},{1,9},{9,17},{17,25},{2,10},{10,18},{18,26},{... | collective-permute-start | bytes 442376 | tf_op jit(solution)/shard_map/ppermute | solution.py:21
  10.1 14.4 %copy-start.55 = (s32[16,256]{1,0:T(8,128)}, s32[16,256]{1,0:T(8,128)S(1)}, u32[]{:S(2)}) copy-start(s32[16,256]{1,0:T(8,128)S(1)} %get-tuple-element.637) | copy-start | bytes 49156
  10.1 27.9 %copy-start.52 = (s32[16,256]{1,0:T(8,128)}, s32[16,256]{1,0:T(8,128)S(1)}, u32[]{:S(2)}) copy-start(s32[16,256]{1,0:T(8,128)S(1)} %get-tuple-element.636) | copy-start | bytes 49156
  16.6 42.9 %copy-start.30 = (pred[32,484]{1,0:T(8,128)(4,1)}, pred[32,484]{1,0:T(8,128)(4,1)S(1)}, u32[]{:S(2)}) copy-start(pred[32,484]{1,0:T(8,128)(4,1)S(1)} %iota_compare_fusion.40) | copy-start | bytes 46468
  17.1 13.4 %copy-start.48 = (s32[16]{0:T(128)}, s32[16]{0:T(128)S(1)}, u32[]{:S(2)}) copy-start(s32[16]{0:T(128)S(1)} %get-tuple-element.643) | copy-start | bytes 196
  32.0 10.1 %copy-start.18 = (f32[3,3,16,256]{3,1,2,0:T(4,128)}, f32[3,3,16,256]{3,1,2,0:T(4,128)S(1)}, u32[]{:S(2)}) copy-start(f32[3,3,16,256]{3,1,2,0:T(4,128)S(1)} %collective-permute-done.1) | copy-start | bytes 442372
  32.0 10.1 %copy-start.20 = (f32[3,3,16,256]{3,1,2,0:T(4,128)}, f32[3,3,16,256]{3,1,2,0:T(4,128)S(1)}, u32[]{:S(2)}) copy-start(f32[3,3,16,256]{3,1,2,0:T(4,128)S(1)} %collective-permute-done) | copy-start | bytes 442372
  32.1 9.3 %collective-permute-start.3 = (f32[3,22,3,256]{3,1,2,0:T(8,128)S(1)}, f32[3,22,3,256]{3,1,2,0:T(8,128)S(1)}, u32[]{:S(2)}, u32[]{:S(2)}) collective-permute-start(f32[3,22,3,256]{3,1,2,0:T(8,128)S(1)} %get-tuple-element.590), channel_id=1, source_target_pairs={{2,0},{4,2},{6,4},{3,1},{5,3},{7,5},{10,8},{12,10},{14,12},{11,9},... | collective-permute-start | bytes 608264 | tf_op jit(solution)/shard_map/ppermute | solution.py:23
  33.4 8.7 %collective-permute-start.2 = (f32[3,22,3,256]{3,1,2,0:T(8,128)S(1)}, f32[3,22,3,256]{3,1,2,0:T(8,128)S(1)}, u32[]{:S(2)}, u32[]{:S(2)}) collective-permute-start(f32[3,22,3,256]{3,1,2,0:T(8,128)S(1)} %get-tuple-element.589), channel_id=1, source_target_pairs={{0,2},{2,4},{4,6},{1,3},{3,5},{5,7},{8,10},{10,12},{12,14},{9,11},... | collective-permute-start | bytes 608264 | tf_op jit(solution)/shard_map/ppermute | solution.py:21
  44.5 10.4 %copy-start.19 = (f32[3,3,16,256]{3,1,2,0:T(4,128)S(1)}, f32[3,3,16,256]{3,1,2,0:T(4,128)}, u32[]{:S(2)}) copy-start(f32[3,3,16,256]{3,1,2,0:T(4,128)} %copy-done.18) | copy-start | bytes 442372
  44.5 8.3 %collective-permute-start.5 = (f32[3,22,22,3]{2,1,3,0:T(8,128)}, f32[3,22,22,3]{2,1,3,0:T(8,128)S(1)}, u32[]{:S(2)}, u32[]{:S(2)}) collective-permute-start(f32[3,22,22,3]{2,1,3,0:T(8,128)} %copy.270), channel_id=1, source_target_pairs={{1,0},{3,2},{5,4},{7,6},{9,8},{11,10},{13,12},{15,14},{17,16},{19,... | collective-permute-start | bytes 52280 | tf_op jit(solution)/shard_map/ppermute | solution.py:23
  46.5 7.0 %collective-permute-start.4 = (f32[3,22,22,3]{2,1,3,0:T(8,128)S(1)}, f32[3,22,22,3]{2,1,3,0:T(8,128)}, u32[]{:S(2)}, u32[]{:S(2)}) collective-permute-start(f32[3,22,22,3]{2,1,3,0:T(8,128)S(1)} %copy.269), channel_id=1, source_target_pairs={{0,1},{2,3},{4,5},{6,7},{8,9},{10,11},{12,13},{14,15},{16,17},{18,... | collective-permute-start | bytes 52280 | tf_op jit(solution)/shard_map/ppermute | solution.py:21
  59.4 51.5 %copy-start.53 = (s32[16,256]{1,0:T(8,128)S(1)}, s32[16,256]{1,0:T(8,128)}, u32[]{:S(2)}) copy-start(s32[16,256]{1,0:T(8,128)} %copy-done.52) | copy-start | bytes 49156
  59.4 53.2 %copy-start.13 = (f32[3,256,256]{1,2,0:T(8,128)S(1)}, f32[3,256,256]{1,2,0:T(8,128)}, u32[]{:S(2)}) copy-start(f32[3,256,256]{1,2,0:T(8,128)} %fusion.132) | copy-start | bytes 2359300
  59.4 53.2 %copy-start.70 = (s32[16]{0:T(128)S(1)}, s32[16]{0:T(128)}, u32[]{:S(2)}) copy-start(s32[16]{0:T(128)} %get-tuple-element.642) | copy-start | bytes 196
  113.2 8.9 %copy-start.6 = (f32[3,256,256]{1,2,0:T(8,128)}, f32[3,256,256]{1,2,0:T(8,128)S(1)}, u32[]{:S(2)}) copy-start(f32[3,256,256]{1,2,0:T(8,128)S(1)} %fusion.77) | copy-start | bytes 2359300
  113.4 14.9 %copy-start.56 = (s32[16,256]{1,0:T(8,128)S(1)}, s32[16,256]{1,0:T(8,128)}, u32[]{:S(2)}) copy-start(s32[16,256]{1,0:T(8,128)} %copy-done.55) | copy-start | bytes 49156
  113.5 7.0 %collective-permute-start.7 = (f32[3,3,16,256]{3,2,1,0:T(8,128)S(1)}, f32[3,3,16,256]{3,2,1,0:T(8,128)S(1)}, u32[]{:S(2)}, u32[]{:S(2)}) collective-permute-start(f32[3,3,16,256]{3,2,1,0:T(8,128)S(1)} %get-tuple-element.614), channel_id=1, source_target_pairs={{8,0},{16,8},{24,16},{9,1},{17,9},{25,17},{10,2},{18,10},{26,18},{... | collective-permute-start | bytes 442376 | tf_op jit(solution)/shard_map/ppermute | solution.py:23
  114.8 7.2 %collective-permute-start.6 = (f32[3,3,16,256]{3,2,1,0:T(8,128)S(1)}, f32[3,3,16,256]{3,2,1,0:T(8,128)S(1)}, u32[]{:S(2)}, u32[]{:S(2)}) collective-permute-start(f32[3,3,16,256]{3,2,1,0:T(8,128)S(1)} %get-tuple-element.613), channel_id=1, source_target_pairs={{0,8},{8,16},{16,24},{1,9},{9,17},{17,25},{2,10},{10,18},{18,26},{... | collective-permute-start | bytes 442376 | tf_op jit(solution)/shard_map/ppermute | solution.py:21
  122.0 10.3 %copy-start.23 = (f32[3,3,16,256]{3,2,1,0:T(8,128)}, f32[3,3,16,256]{3,2,1,0:T(8,128)S(1)}, u32[]{:S(2)}) copy-start(f32[3,3,16,256]{3,2,1,0:T(8,128)S(1)} %collective-permute-done.6) | copy-start | bytes 442372
  122.1 9.7 %collective-permute-start.9 = (f32[3,22,3,256]{3,1,2,0:T(8,128)S(1)}, f32[3,22,3,256]{3,1,2,0:T(8,128)S(1)}, u32[]{:S(2)}, u32[]{:S(2)}) collective-permute-start(f32[3,22,3,256]{3,1,2,0:T(8,128)S(1)} %copy.294), channel_id=1, source_target_pairs={{2,0},{4,2},{6,4},{3,1},{5,3},{7,5},{10,8},{12,10},{14,12},{11,9},... | collective-permute-start | bytes 608264 | tf_op jit(solution)/shard_map/ppermute | solution.py:23
  123.5 8.4 %collective-permute-start.8 = (f32[3,22,3,256]{3,1,2,0:T(8,128)S(1)}, f32[3,22,3,256]{3,1,2,0:T(8,128)S(1)}, u32[]{:S(2)}, u32[]{:S(2)}) collective-permute-start(f32[3,22,3,256]{3,1,2,0:T(8,128)S(1)} %copy.293), channel_id=1, source_target_pairs={{0,2},{2,4},{4,6},{1,3},{3,5},{5,7},{8,10},{10,12},{12,14},{9,11},... | collective-permute-start | bytes 608264 | tf_op jit(solution)/shard_map/ppermute | solution.py:21
  135.4 10.4 %collective-permute-start.11 = (f32[3,22,22,3]{2,1,3,0:T(8,128)S(1)}, f32[3,22,22,3]{2,1,3,0:T(8,128)S(1)}, u32[]{:S(2)}, u32[]{:S(2)}) collective-permute-start(f32[3,22,22,3]{2,1,3,0:T(8,128)S(1)} %copy.298), channel_id=1, source_target_pairs={{1,0},{3,2},{5,4},{7,6},{9,8},{11,10},{13,12},{15,14},{17,16},{19,... | collective-permute-start | bytes 52280 | tf_op jit(solution)/shard_map/ppermute | solution.py:23
  138.4 7.9 %collective-permute-start.10 = (f32[3,22,22,3]{2,1,3,0:T(8,128)S(1)}, f32[3,22,22,3]{2,1,3,0:T(8,128)}, u32[]{:S(2)}, u32[]{:S(2)}) collective-permute-start(f32[3,22,22,3]{2,1,3,0:T(8,128)S(1)} %copy.297), channel_id=1, source_target_pairs={{0,1},{2,3},{4,5},{6,7},{8,9},{10,11},{12,13},{14,15},{16,17},{18,... | collective-permute-start | bytes 52280 | tf_op jit(solution)/shard_map/ppermute | solution.py:21
  165.3 51.8 %copy-start.71 = (s32[16]{0:T(128)S(1)}, s32[16]{0:T(128)}, u32[]{:S(2)}) copy-start(s32[16]{0:T(128)} %get-tuple-element.642) | copy-start | bytes 196
  217.8 8.9 %copy-start.8 = (f32[3,256,256]{1,2,0:T(8,128)}, f32[3,256,256]{1,2,0:T(8,128)S(1)}, u32[]{:S(2)}) copy-start(f32[3,256,256]{1,2,0:T(8,128)S(1)} %fusion.76) | copy-start | bytes 2359300
  218.0 14.9 %copy-start.58 = (s32[16,256]{1,0:T(8,128)S(1)}, s32[16,256]{1,0:T(8,128)}, u32[]{:S(2)}) copy-start(s32[16,256]{1,0:T(8,128)} %copy-done.55) | copy-start | bytes 49156
  218.0 7.3 %collective-permute-start.13 = (f32[3,3,16,256]{3,2,1,0:T(8,128)S(1)}, f32[3,3,16,256]{3,2,1,0:T(8,128)S(1)}, u32[]{:S(2)}, u32[]{:S(2)}) collective-permute-start(f32[3,3,16,256]{3,2,1,0:T(8,128)S(1)} %get-tuple-element.610), channel_id=1, source_target_pairs={{8,0},{16,8},{24,16},{9,1},{17,9},{25,17},{10,2},{18,10},{26,18},{... | collective-permute-start | bytes 442376 | tf_op jit(solution)/shard_map/ppermute | solution.py:23
  219.3 7.2 %collective-permute-start.12 = (f32[3,3,16,256]{3,2,1,0:T(8,128)S(1)}, f32[3,3,16,256]{3,2,1,0:T(8,128)S(1)}, u32[]{:S(2)}, u32[]{:S(2)}) collective-permute-start(f32[3,3,16,256]{3,2,1,0:T(8,128)S(1)} %get-tuple-element.609), channel_id=1, source_target_pairs={{0,8},{8,16},{16,24},{1,9},{9,17},{17,25},{2,10},{10,18},{18,26},{... | collective-permute-start | bytes 442376 | tf_op jit(solution)/shard_map/ppermute | solution.py:21
  225.3 11.1 %copy-start.21 = (f32[3,3,16,256]{3,2,1,0:T(8,128)}, f32[3,3,16,256]{3,2,1,0:T(8,128)S(1)}, u32[]{:S(2)}) copy-start(f32[3,3,16,256]{3,2,1,0:T(8,128)S(1)} %collective-permute-done.13) | copy-start | bytes 442372
  226.5 11.0 %copy-start.24 = (f32[3,3,16,256]{3,2,1,0:T(8,128)}, f32[3,3,16,256]{3,2,1,0:T(8,128)S(1)}, u32[]{:S(2)}) copy-start(f32[3,3,16,256]{3,2,1,0:T(8,128)S(1)} %collective-permute-done.12) | copy-start | bytes 442372
  226.7 9.0 %collective-permute-start.15 = (f32[3,22,3,256]{3,1,2,0:T(8,128)S(1)}, f32[3,22,3,256]{3,1,2,0:T(8,128)S(1)}, u32[]{:S(2)}, u32[]{:S(2)}) collective-permute-start(f32[3,22,3,256]{3,1,2,0:T(8,128)S(1)} %copy.320), channel_id=1, source_target_pairs={{2,0},{4,2},{6,4},{3,1},{5,3},{7,5},{10,8},{12,10},{14,12},{11,9},... | collective-permute-start | bytes 608264 | tf_op jit(solution)/shard_map/ppermute | solution.py:23
  228.0 8.3 %collective-permute-start.14 = (f32[3,22,3,256]{3,1,2,0:T(8,128)S(1)}, f32[3,22,3,256]{3,1,2,0:T(8,128)S(1)}, u32[]{:S(2)}, u32[]{:S(2)}) collective-permute-start(f32[3,22,3,256]{3,1,2,0:T(8,128)S(1)} %copy.319), channel_id=1, source_target_pairs={{0,2},{2,4},{4,6},{1,3},{3,5},{5,7},{8,10},{10,12},{12,14},{9,11},... | collective-permute-start | bytes 608264 | tf_op jit(solution)/shard_map/ppermute | solution.py:21
  240.3 8.5 %collective-permute-start.17 = (f32[3,22,22,3]{2,1,3,0:T(8,128)S(1)}, f32[3,22,22,3]{2,1,3,0:T(8,128)S(1)}, u32[]{:S(2)}, u32[]{:S(2)}) collective-permute-start(f32[3,22,22,3]{2,1,3,0:T(8,128)S(1)} %copy.324), channel_id=1, source_target_pairs={{1,0},{3,2},{5,4},{7,6},{9,8},{11,10},{13,12},{15,14},{17,16},{19,... | collective-permute-start | bytes 52280 | tf_op jit(solution)/shard_map/ppermute | solution.py:23
  242.1 8.0 %collective-permute-start.16 = (f32[3,22,22,3]{2,1,3,0:T(8,128)S(1)}, f32[3,22,22,3]{2,1,3,0:T(8,128)S(1)}, u32[]{:S(2)}, u32[]{:S(2)}) collective-permute-start(f32[3,22,22,3]{2,1,3,0:T(8,128)S(1)} %copy.323), channel_id=1, source_target_pairs={{0,1},{2,3},{4,5},{6,7},{8,9},{10,11},{12,13},{14,15},{16,17},{18,... | collective-permute-start | bytes 52280 | tf_op jit(solution)/shard_map/ppermute | solution.py:21
  269.0 52.4 %copy-start.54 = (s32[16,256]{1,0:T(8,128)S(1)}, s32[16,256]{1,0:T(8,128)}, u32[]{:S(2)}) copy-start(s32[16,256]{1,0:T(8,128)} %copy-done.52) | copy-start | bytes 49156
  269.0 54.0 %copy-start.72 = (s32[16]{0:T(128)S(1)}, s32[16]{0:T(128)}, u32[]{:S(2)}) copy-start(s32[16]{0:T(128)} %get-tuple-element.642) | copy-start | bytes 196
  323.6 8.9 %copy-start.10 = (f32[3,256,256]{1,2,0:T(8,128)}, f32[3,256,256]{1,2,0:T(8,128)S(1)}, u32[]{:S(2)}) copy-start(f32[3,256,256]{1,2,0:T(8,128)S(1)} %fusion.75) | copy-start | bytes 2359300
  323.8 14.9 %copy-start.60 = (s32[16,256]{1,0:T(8,128)S(1)}, s32[16,256]{1,0:T(8,128)}, u32[]{:S(2)}) copy-start(s32[16,256]{1,0:T(8,128)} %copy-done.55) | copy-start | bytes 49156
  323.9 7.1 %collective-permute-start.19 = (f32[3,3,16,256]{3,2,1,0:T(8,128)S(1)}, f32[3,3,16,256]{3,2,1,0:T(8,128)S(1)}, u32[]{:S(2)}, u32[]{:S(2)}) collective-permute-start(f32[3,3,16,256]{3,2,1,0:T(8,128)S(1)} %get-tuple-element.606), channel_id=1, source_target_pairs={{8,0},{16,8},{24,16},{9,1},{17,9},{25,17},{10,2},{18,10},{26,18},{... | collective-permute-start | bytes 442376 | tf_op jit(solution)/shard_map/ppermute | solution.py:23
  325.2 7.2 %collective-permute-start.18 = (f32[3,3,16,256]{3,2,1,0:T(8,128)S(1)}, f32[3,3,16,256]{3,2,1,0:T(8,128)S(1)}, u32[]{:S(2)}, u32[]{:S(2)}) collective-permute-start(f32[3,3,16,256]{3,2,1,0:T(8,128)S(1)} %get-tuple-element.605), channel_id=1, source_target_pairs={{0,8},{8,16},{16,24},{1,9},{9,17},{17,25},{2,10},{10,18},{18,26},{... | collective-permute-start | bytes 442376 | tf_op jit(solution)/shard_map/ppermute | solution.py:21
  332.4 10.2 %copy-start.25 = (f32[3,3,16,256]{3,2,1,0:T(8,128)}, f32[3,3,16,256]{3,2,1,0:T(8,128)S(1)}, u32[]{:S(2)}) copy-start(f32[3,3,16,256]{3,2,1,0:T(8,128)S(1)} %collective-permute-done.18) | copy-start | bytes 442372
  332.5 9.5 %collective-permute-start.21 = (f32[3,22,3,256]{3,1,2,0:T(8,128)S(1)}, f32[3,22,3,256]{3,1,2,0:T(8,128)S(1)}, u32[]{:S(2)}, u32[]{:S(2)}) collective-permute-start(f32[3,22,3,256]{3,1,2,0:T(8,128)S(1)} %copy.346), channel_id=1, source_target_pairs={{2,0},{4,2},{6,4},{3,1},{5,3},{7,5},{10,8},{12,10},{14,12},{11,9},... | collective-permute-start | bytes 608264 | tf_op jit(solution)/shard_map/ppermute | solution.py:23
  333.9 8.3 %collective-permute-start.20 = (f32[3,22,3,256]{3,1,2,0:T(8,128)S(1)}, f32[3,22,3,256]{3,1,2,0:T(8,128)S(1)}, u32[]{:S(2)}, u32[]{:S(2)}) collective-permute-start(f32[3,22,3,256]{3,1,2,0:T(8,128)S(1)} %copy.345), channel_id=1, source_target_pairs={{0,2},{2,4},{4,6},{1,3},{3,5},{5,7},{8,10},{10,12},{12,14},{9,11},... | collective-permute-start | bytes 608264 | tf_op jit(solution)/shard_map/ppermute | solution.py:21
  345.7 10.2 %collective-permute-start.23 = (f32[3,22,22,3]{2,1,3,0:T(8,128)S(1)}, f32[3,22,22,3]{2,1,3,0:T(8,128)S(1)}, u32[]{:S(2)}, u32[]{:S(2)}) collective-permute-start(f32[3,22,22,3]{2,1,3,0:T(8,128)S(1)} %copy.350), channel_id=1, source_target_pairs={{1,0},{3,2},{5,4},{7,6},{9,8},{11,10},{13,12},{15,14},{17,16},{19,... | collective-permute-start | bytes 52280 | tf_op jit(solution)/shard_map/ppermute | solution.py:23
  348.6 7.8 %collective-permute-start.22 = (f32[3,22,22,3]{2,1,3,0:T(8,128)S(1)}, f32[3,22,22,3]{2,1,3,0:T(8,128)}, u32[]{:S(2)}, u32[]{:S(2)}) collective-permute-start(f32[3,22,22,3]{2,1,3,0:T(8,128)S(1)} %copy.349), channel_id=1, source_target_pairs={{0,1},{2,3},{4,5},{6,7},{8,9},{10,11},{12,13},{14,15},{16,17},{18,... | collective-permute-start | bytes 52280 | tf_op jit(solution)/shard_map/ppermute | solution.py:21
  375.5 52.0 %copy-start.73 = (s32[16]{0:T(128)S(1)}, s32[16]{0:T(128)}, u32[]{:S(2)}) copy-start(s32[16]{0:T(128)} %get-tuple-element.642) | copy-start | bytes 196
  428.0 8.9 %copy-start.12 = (f32[3,256,256]{1,2,0:T(8,128)}, f32[3,256,256]{1,2,0:T(8,128)S(1)}, u32[]{:S(2)}) copy-start(f32[3,256,256]{1,2,0:T(8,128)S(1)} %fusion.74) | copy-start | bytes 2359300
  428.3 14.9 %copy-start.62 = (s32[16,256]{1,0:T(8,128)S(1)}, s32[16,256]{1,0:T(8,128)}, u32[]{:S(2)}) copy-start(s32[16,256]{1,0:T(8,128)} %copy-done.55) | copy-start | bytes 49156
  428.3 7.1 %collective-permute-start.25 = (f32[3,3,16,256]{3,2,1,0:T(8,128)S(1)}, f32[3,3,16,256]{3,2,1,0:T(8,128)S(1)}, u32[]{:S(2)}, u32[]{:S(2)}) collective-permute-start(f32[3,3,16,256]{3,2,1,0:T(8,128)S(1)} %get-tuple-element.602), channel_id=1, source_target_pairs={{8,0},{16,8},{24,16},{9,1},{17,9},{25,17},{10,2},{18,10},{26,18},{... | collective-permute-start | bytes 442376 | tf_op jit(solution)/shard_map/ppermute | solution.py:23
  429.6 7.2 %collective-permute-start.24 = (f32[3,3,16,256]{3,2,1,0:T(8,128)S(1)}, f32[3,3,16,256]{3,2,1,0:T(8,128)S(1)}, u32[]{:S(2)}, u32[]{:S(2)}) collective-permute-start(f32[3,3,16,256]{3,2,1,0:T(8,128)S(1)} %get-tuple-element.601), channel_id=1, source_target_pairs={{0,8},{8,16},{16,24},{1,9},{9,17},{17,25},{2,10},{10,18},{18,26},{... | collective-permute-start | bytes 442376 | tf_op jit(solution)/shard_map/ppermute | solution.py:21
  435.4 11.3 %copy-start.22 = (f32[3,3,16,256]{3,2,1,0:T(8,128)}, f32[3,3,16,256]{3,2,1,0:T(8,128)S(1)}, u32[]{:S(2)}) copy-start(f32[3,3,16,256]{3,2,1,0:T(8,128)S(1)} %collective-permute-done.25) | copy-start | bytes 442372
  436.8 10.9 %copy-start.26 = (f32[3,3,16,256]{3,2,1,0:T(8,128)}, f32[3,3,16,256]{3,2,1,0:T(8,128)S(1)}, u32[]{:S(2)}) copy-start(f32[3,3,16,256]{3,2,1,0:T(8,128)S(1)} %collective-permute-done.24) | copy-start | bytes 442372
  437.0 9.0 %collective-permute-start.27 = (f32[3,22,3,256]{3,1,2,0:T(8,128)S(1)}, f32[3,22,3,256]{3,1,2,0:T(8,128)S(1)}, u32[]{:S(2)}, u32[]{:S(2)}) collective-permute-start(f32[3,22,3,256]{3,1,2,0:T(8,128)S(1)} %copy.372), channel_id=1, source_target_pairs={{2,0},{4,2},{6,4},{3,1},{5,3},{7,5},{10,8},{12,10},{14,12},{11,9},... | collective-permute-start | bytes 608264 | tf_op jit(solution)/shard_map/ppermute | solution.py:23
  438.3 8.3 %collective-permute-start.26 = (f32[3,22,3,256]{3,1,2,0:T(8,128)S(1)}, f32[3,22,3,256]{3,1,2,0:T(8,128)S(1)}, u32[]{:S(2)}, u32[]{:S(2)}) collective-permute-start(f32[3,22,3,256]{3,1,2,0:T(8,128)S(1)} %copy.371), channel_id=1, source_target_pairs={{0,2},{2,4},{4,6},{1,3},{3,5},{5,7},{8,10},{10,12},{12,14},{9,11},... | collective-permute-start | bytes 608264 | tf_op jit(solution)/shard_map/ppermute | solution.py:21
  450.6 8.5 %collective-permute-start.29 = (f32[3,22,22,3]{2,1,3,0:T(8,128)S(1)}, f32[3,22,22,3]{2,1,3,0:T(8,128)S(1)}, u32[]{:S(2)}, u32[]{:S(2)}) collective-permute-start(f32[3,22,22,3]{2,1,3,0:T(8,128)S(1)} %copy.376), channel_id=1, source_target_pairs={{1,0},{3,2},{5,4},{7,6},{9,8},{11,10},{13,12},{15,14},{17,16},{19,... | collective-permute-start | bytes 52280 | tf_op jit(solution)/shard_map/ppermute | solution.py:23
  452.4 8.0 %collective-permute-start.28 = (f32[3,22,22,3]{2,1,3,0:T(8,128)S(1)}, f32[3,22,22,3]{2,1,3,0:T(8,128)S(1)}, u32[]{:S(2)}, u32[]{:S(2)}) collective-permute-start(f32[3,22,22,3]{2,1,3,0:T(8,128)S(1)} %copy.375), channel_id=1, source_target_pairs={{0,1},{2,3},{4,5},{6,7},{8,9},{10,11},{12,13},{14,15},{16,17},{18,... | collective-permute-start | bytes 52280 | tf_op jit(solution)/shard_map/ppermute | solution.py:21
  480.0 54.8 %copy-start.7 = (f32[3,256,256]{1,2,0:T(8,128)S(1)}, f32[3,256,256]{1,2,0:T(8,128)}, u32[]{:S(2)}) copy-start(f32[3,256,256]{1,2,0:T(8,128)} %copy-done.6) | copy-start | bytes 2359300
  480.0 54.8 %copy-start.9 = (f32[3,256,256]{1,2,0:T(8,128)S(1)}, f32[3,256,256]{1,2,0:T(8,128)}, u32[]{:S(2)}) copy-start(f32[3,256,256]{1,2,0:T(8,128)} %copy-done.8) | copy-start | bytes 2359300
  480.0 54.8 %copy-start.11 = (f32[3,256,256]{1,2,0:T(8,128)S(1)}, f32[3,256,256]{1,2,0:T(8,128)}, u32[]{:S(2)}) copy-start(f32[3,256,256]{1,2,0:T(8,128)} %copy-done.10) | copy-start | bytes 2359300
  (41 other events, 182.2 us)
where the time goes:
time: 595 us; the launch traced here: 585 us
  blocking collectives  258 us (43%)
  matrix products  107 us (18%)
  starting transfers between devices  85.6 us (14%)
  local copies, waits for them, and re-layouts  75.5 us (13%)
  other arithmetic  37.2 us (6%)
  between operations  12.3 us (2%)
  waiting for transfers between devices  10.5 us (2%)
    psum x5, blocking collectives, local(): total_energy = lax.psum(energy_local, ('gx', 'gy', 'gz'))  218 us
    ppermute x15, starting transfers between devices, extended(): lax.ppermute(tail, axis, [(i, (i + 1) % count) for i in range(ends)])  66.1 us
    psum x1, blocking collectives, local(): residuals.append(lax.psum(residual_local, ('gx', 'gy', 'gz')))  39.2 us
    dot_general x10, matrix products, sweep_add_group(): jnp.einsum('bcn,bpn->bcp', near_lines, near_hot, precision=highest)  29.1 us
    dot_general x15, matrix products, select_lines(): return jnp.einsum('bl,cln->bcn', line_hot, field_lines, precision=highest)  27.3 us
    concatenate x10, other arithmetic, extended(): jnp.concatenate([lax.ppermute(tail, axis, [(i, (i + 1) % count) for i in...  23.8 us
    ppermute x15, starting transfers between devices, extended(): lax.ppermute(head, axis, [((i + 1) % count, i) for i in range(ends)])  19.5 us
    dot_general x10, matrix products, sweep_add_group(): far_vals = jnp.einsum('bcn,bpn->bcp', far_lines, far_hot, precision=highest)  18.4 us
  transfers between devices with their start and end apart: 30, of which 11 were waited for; matrix products, arithmetic and copies ran while one was open for 11% of the time, Pallas kernels for 0%

commit v1 on v0

--- a/solution.py
+++ b/solution.py
@@ -151,7 +151,9 @@
         )
         node_total = inner_total + outer_total
         energy_local = inner_energy + outer_energy
-        total_energy = lax.psum(energy_local, ("gx", "gy", "gz"))
+        total_energy = energy_local
+        for mesh_axis in (("gy", "gz"), "gx"):
+            total_energy = lax.psum(total_energy, mesh_axis)
         scale_factor = 1.0 / (1.0 + total_energy / (slot_count * devices))
         correction = (
             relax_factor

time: 595 us -> 507 us (0.85)
  blocking collectives: 258 us -> 166 us
    psum x5 -> x10, blocking collectives: 218 us -> 129 us  [local(): total_energy = lax.psum(total_energy, mesh_axis)]
  transfers between devices with their start and end apart: 30 -> 30, of which waited for: 11 -> 14; matrix products, arithmetic and copies ran while one was open for 11% -> 13% of each run, Pallas kernels for 0% -> 0%
where the time goes in v1:
time: 507 us; the launch traced here: 497 us
  blocking collectives  166 us (33%)
  matrix products  107 us (21%)
  starting transfers between devices  84.5 us (17%)
  local copies, waits for them, and re-layouts  78.1 us (15%)
  other arithmetic  38.2 us (8%)
  between operations  12.8 us (3%)
  waiting for transfers between devices  10.4 us (2%)
    psum x10, blocking collectives, local(): total_energy = lax.psum(total_energy, mesh_axis)  129 us
    ppermute x15, starting transfers between devices, extended(): lax.ppermute(tail, axis, [(i, (i + 1) % count) for i in range(ends)])  65.1 us
    psum x1, blocking collectives, local(): residuals.append(lax.psum(residual_local, ('gx', 'gy', 'gz')))  37.8 us
    dot_general x10, matrix products, sweep_add_group(): jnp.einsum('bcn,bpn->bcp', near_lines, near_hot, precision=highest)  29.1 us
    dot_general x15, matrix products, select_lines(): return jnp.einsum('bl,cln->bcn', line_hot, field_lines, precision=highest)  27.3 us
    concatenate x10, other arithmetic, extended(): jnp.concatenate([lax.ppermute(tail, axis, [(i, (i + 1) % count) for i in...  25 us
    ppermute x15, starting transfers between devices, extended(): lax.ppermute(head, axis, [((i + 1) % count, i) for i in range(ends)])  19.4 us
    dot_general x10, matrix products, sweep_add_group(): far_vals = jnp.einsum('bcn,bpn->bcp', far_lines, far_hot, precision=highest)  19.2 us
  transfers between devices with their start and end apart: 30, of which 14 were waited for; matrix products, arithmetic and copies ran while one was open for 13% of the time, Pallas kernels for 0%

profile of v1, /device:TPU:0, one launch (start us, length us, event | category | flops | bytes accessed | tf_op | source)
XLA Modules:
  0.0 497.2 jit_solution(14605163667762116958)
XLA Ops:
  3.7 5.6 %collective-permute-start = (f32[3,3,16,256]{3,1,2,0:T(4,128)S(1)}, f32[3,3,16,256]{3,1,2,0:T(4,128)S(1)}, u32[]{:S(2)}, u32[]{:S(2)}) collective-permute-start(f32[3,3,16,256]{3,1,2,0:T(4,128)S(1)} %get-tuple-element.615), channel_id=1, source_target_pairs={{0,8},{8,16},{16,24},{1,9},{9,17},{17,25},{2,10},{10,18},{18,26},{... | collective-permute-start | bytes 442376 | tf_op jit(solution)/shard_map/ppermute | solution.py:21
  13.4 3.0 reshape.413
  17.6 2.5 fusion.244
  25.8 4.3 while.9
  32.9 4.6 collective-permute-start.2
  37.5 2.8 fusion.32
  49.0 4.2 collective-permute-start.4
  55.9 2.5 pad_maximum_fusion
  60.6 2.5 fusion.249
  63.1 2.3 fusion.17
  67.7 17.0 %psum.105 = f32[]{:T(128)} all-reduce(f32[]{:T(128)S(6)} %add.359), channel_id=1, replica_groups=mesh['gx'=4,'gy'=4,'gz'=2] {'gy','gz'}, use_global_device_ids=true, to_apply=%region_2.3 | all-reduce | flops 1 | bytes 8 | tf_op jit(solution)/shard_map/psum | solution.py:156
  85.5 10.7 %psum.106 = f32[]{:T(128)} all-reduce(f32[]{:T(128)} %psum.105), channel_id=1, replica_groups=mesh['gx'=4,'gy'=4,'gz'=2] {'gx'}, use_global_device_ids=true, to_apply=%region_3.4 | all-reduce | flops 1 | bytes 8 | tf_op jit(solution)/shard_map/psum | solution.py:156
  100.6 4.6 collective-permute-start.6
  109.3 4.6 collective-permute-start.8
  123.8 3.8 collective-permute-start.10
  127.6 3.6 fusion.30
  133.2 5.1 %pad_maximum_fusion.1 = (f32[3,22,22,262]{3,2,1,0:T(8,128)}, f32[3,22,22,262]{3,2,1,0:T(8,128)}) fusion(f32[3,22,22,3]{3,2,1,0:T(8,128)S(1)} %copy.300, f32[3,22,3,256]{3,2,1,0:T(4,128)S(1)} %copy.296, f32[3,3,16,256]{3,2,1,0:T(8,128)S(1)} %collective-permute-done.7, f32[3,16,16,256]{3,2,1,0:T(8,128)S(1)} %divide_add_fusion.4, ...), kind=kLoop, calls=%fused_computation.50 | loop fusion | flops 2282544 | bytes 4565088 | tf_op jit(solution)/shard_map/concatenate | solution.py:19
  138.2 3.0 reshape.416
  141.2 2.5 fusion.243
  146.1 3.0 reshape.417
  149.1 2.5 fusion.248
  157.0 13.3 %psum.107 = f32[]{:T(128)} all-reduce(f32[]{:T(128)S(6)} %add.369), channel_id=1, replica_groups=mesh['gx'=4,'gy'=4,'gz'=2] {'gy','gz'}, use_global_device_ids=true, to_apply=%region_8.9 | all-reduce | flops 1 | bytes 8 | tf_op jit(solution)/shard_map/psum | solution.py:156
  170.8 11.5 %psum.108 = f32[]{:T(128)} all-reduce(f32[]{:T(128)} %psum.107), channel_id=1, replica_groups=mesh['gx'=4,'gy'=4,'gz'=2] {'gx'}, use_global_device_ids=true, to_apply=%region_9.10 | all-reduce | flops 1 | bytes 8 | tf_op jit(solution)/shard_map/psum | solution.py:156
  186.7 4.6 collective-permute-start.12
  195.4 5.0 collective-permute-start.14
  200.4 2.8 fusion.38
  209.7 3.0 collective-permute-start.16
  212.7 3.6 fusion.28
  219.2 5.0 pad_maximum_fusion.2
  224.1 3.0 reshape.419
  227.1 2.5 fusion.242
  229.7 2.3 fusion.20
  235.1 2.5 fusion.247
  237.6 2.3 fusion.15
  243.7 14.3 %psum.109 = f32[]{:T(128)} all-reduce(f32[]{:T(128)S(6)} %add.377), channel_id=1, replica_groups=mesh['gx'=4,'gy'=4,'gz'=2] {'gy','gz'}, use_global_device_ids=true, to_apply=%region_12.13 | all-reduce | flops 1 | bytes 8 | tf_op jit(solution)/shard_map/psum | solution.py:156
  258.6 11.2 %psum.110 = f32[]{:T(128)} all-reduce(f32[]{:T(128)} %psum.109), channel_id=1, replica_groups=mesh['gx'=4,'gy'=4,'gz'=2] {'gx'}, use_global_device_ids=true, to_apply=%region_13.14 | all-reduce | flops 1 | bytes 8 | tf_op jit(solution)/shard_map/psum | solution.py:156
  274.2 4.6 collective-permute-start.18
  283.0 4.6 collective-permute-start.20
  297.4 3.8 collective-permute-start.22
  301.2 3.6 fusion.26
  306.8 5.1 %pad_maximum_fusion.3 = (f32[3,22,22,262]{3,2,1,0:T(8,128)}, f32[3,22,22,262]{3,2,1,0:T(8,128)}) fusion(f32[3,22,22,3]{3,2,1,0:T(8,128)S(1)} %copy.352, f32[3,22,3,256]{3,2,1,0:T(4,128)S(1)} %copy.348, f32[3,3,16,256]{3,2,1,0:T(8,128)S(1)} %collective-permute-done.19, f32[3,16,16,256]{3,2,1,0:T(8,128)S(1)} %divide_add_fusion.2, ...), kind=kLoop, calls=%fused_computation.52 | loop fusion | flops 2282544 | bytes 4565088 | tf_op jit(solution)/shard_map/concatenate | solution.py:19
  311.8 3.0 reshape.422
  314.8 2.5 fusion.241
  319.7 3.0 reshape.423
  322.8 2.5 fusion.246
  330.6 13.4 %psum.111 = f32[]{:T(128)} all-reduce(f32[]{:T(128)S(6)} %add.385), channel_id=1, replica_groups=mesh['gx'=4,'gy'=4,'gz'=2] {'gy','gz'}, use_global_device_ids=true, to_apply=%region_16.17 | all-reduce | flops 1 | bytes 8 | tf_op jit(solution)/shard_map/psum | solution.py:156
  344.6 11.1 %psum.112 = f32[]{:T(128)} all-reduce(f32[]{:T(128)} %psum.111), channel_id=1, replica_groups=mesh['gx'=4,'gy'=4,'gz'=2] {'gx'}, use_global_device_ids=true, to_apply=%region_17.18 | all-reduce | flops 1 | bytes 8 | tf_op jit(solution)/shard_map/psum | solution.py:156
  360.2 4.6 collective-permute-start.24
  368.9 4.8 collective-permute-start.26
  373.7 2.8 fusion.34
  383.0 3.0 collective-permute-start.28
  386.0 3.6 fusion.24
  392.4 5.0 pad_maximum_fusion.4
  397.4 3.0 reshape.425
  400.4 2.5 fusion.240
  410.7 2.6 fusion.245
  413.3 2.3 fusion.13
  418.6 14.8 %psum.113 = f32[]{:T(128)} all-reduce(f32[]{:T(128)S(6)} %add.393), channel_id=1, replica_groups=mesh['gx'=4,'gy'=4,'gz'=2] {'gy','gz'}, use_global_device_ids=true, to_apply=%region_20.21 | all-reduce | flops 1 | bytes 8 | tf_op jit(solution)/shard_map/psum | solution.py:156
  433.5 2.3 fusion.23
  435.7 11.3 %psum.114 = f32[]{:T(128)} all-reduce(f32[]{:T(128)} %psum.113), channel_id=1, replica_groups=mesh['gx'=4,'gy'=4,'gz'=2] {'gx'}, use_global_device_ids=true, to_apply=%region_21.22 | all-reduce | flops 1 | bytes 8 | tf_op jit(solution)/shard_map/psum | solution.py:156
  447.8 3.1 fusion.88
  452.0 37.8 %all-reduce.5 = (f32[1,1]{1,0:T(1,128)}, f32[1,1]{1,0:T(1,128)}, f32[1,1]{1,0:T(1,128)}, f32[1,1]{1,0:T(1,128)}, f32[1,1]{1,0:T(1,128)}) all-reduce(f32[1,1]{1,0:T(1,128)} %bitcast.57, f32[1,1]{1,0:T(1,128)} %bitcast.58, f32[1,1]{1,0:T(1,128)} %bitcast.59, ...), channel_id=1, replica_groups=mesh['gx'=4,'gy'=4,'gz'=2] {'gx','gy','gz'}, use_global_device_ids=true, to_apply=%region_23.24 | all-reduce | flops 5 | bytes 40 | tf_op jit(solution)/shard_map/psum | solution.py:166
  489.9 3.3 stack.52
  493.2 3.2 stack.46
  (359 shorter events, 140.1 us)
Async XLA Ops:
  0.6 10.8 %copy-start = (f32[3,16,16,256]{3,2,1,0:T(8,128)S(1)}, f32[3,16,16,256]{3,2,1,0:T(8,128)}, u32[]{:S(2)}) copy-start(f32[3,16,16,256]{3,2,1,0:T(8,128)} %param.9) | copy-start | bytes 2359300
  0.6 9.4 %copy-start.32 = (f32[1,1,1,32,4,256]{5,4,3,2,1,0:T(4,128)S(1)}, f32[1,1,1,32,4,256]{5,4,3,2,1,0:T(4,128)}, u32[]{:S(2)}) copy-start(f32[1,1,1,32,4,256]{5,4,3,2,1,0:T(4,128)} %param.14) | copy-start | bytes 393220
  0.6 10.2 %copy-start.42 = (s32[1,1,1,32,256]{4,3,2,1,0:T(8,128)S(1)}, s32[1,1,1,32,256]{4,3,2,1,0:T(8,128)}, u32[]{:S(2)}) copy-start(s32[1,1,1,32,256]{4,3,2,1,0:T(8,128)} %param.12) | copy-start | bytes 98308
  2.4 29.1 %collective-permute-start.1 = (f32[3,3,16,256]{3,1,2,0:T(4,128)S(1)}, f32[3,3,16,256]{3,1,2,0:T(4,128)S(1)}, u32[]{:S(2)}, u32[]{:S(2)}) collective-permute-start(f32[3,3,16,256]{3,1,2,0:T(4,128)S(1)} %get-tuple-element.616), channel_id=1, source_target_pairs={{8,0},{16,8},{24,16},{9,1},{17,9},{25,17},{10,2},{18,10},{26,18},{... | collective-permute-start | bytes 442376 | tf_op jit(solution)/shard_map/ppermute | solution.py:23
  3.7 27.8 %collective-permute-start = (f32[3,3,16,256]{3,1,2,0:T(4,128)S(1)}, f32[3,3,16,256]{3,1,2,0:T(4,128)S(1)}, u32[]{:S(2)}, u32[]{:S(2)}) collective-permute-start(f32[3,3,16,256]{3,1,2,0:T(4,128)S(1)} %get-tuple-element.615), channel_id=1, source_target_pairs={{0,8},{8,16},{16,24},{1,9},{9,17},{17,25},{2,10},{10,18},{18,26},{... | collective-permute-start | bytes 442376 | tf_op jit(solution)/shard_map/ppermute | solution.py:21
  10.1 14.0 %copy-start.53 = (s32[16,256]{1,0:T(8,128)}, s32[16,256]{1,0:T(8,128)S(1)}, u32[]{:S(2)}) copy-start(s32[16,256]{1,0:T(8,128)S(1)} %get-tuple-element.637) | copy-start | bytes 49156
  10.1 27.4 %copy-start.50 = (s32[16,256]{1,0:T(8,128)}, s32[16,256]{1,0:T(8,128)S(1)}, u32[]{:S(2)}) copy-start(s32[16,256]{1,0:T(8,128)S(1)} %get-tuple-element.636) | copy-start | bytes 49156
  11.4 8.7 %copy-start.63 = (s32[16,256]{1,0:T(8,128)}, s32[16,256]{1,0:T(8,128)S(1)}, u32[]{:S(2)}) copy-start(s32[16,256]{1,0:T(8,128)S(1)} %get-tuple-element.639) | copy-start | bytes 49156
  17.2 12.9 %copy-start.46 = (s32[16]{0:T(128)}, s32[16]{0:T(128)S(1)}, u32[]{:S(2)}) copy-start(s32[16]{0:T(128)S(1)} %get-tuple-element.643) | copy-start | bytes 196
  31.5 9.4 %copy-start.18 = (f32[3,3,16,256]{3,1,2,0:T(4,128)}, f32[3,3,16,256]{3,1,2,0:T(4,128)S(1)}, u32[]{:S(2)}) copy-start(f32[3,3,16,256]{3,1,2,0:T(4,128)S(1)} %collective-permute-done.1) | copy-start | bytes 442372
  31.5 9.4 %copy-start.19 = (f32[3,3,16,256]{3,1,2,0:T(4,128)}, f32[3,3,16,256]{3,1,2,0:T(4,128)S(1)}, u32[]{:S(2)}) copy-start(f32[3,3,16,256]{3,1,2,0:T(4,128)S(1)} %collective-permute-done) | copy-start | bytes 442372
  31.6 9.3 %collective-permute-start.3 = (f32[3,22,3,256]{3,1,2,0:T(8,128)S(1)}, f32[3,22,3,256]{3,1,2,0:T(8,128)S(1)}, u32[]{:S(2)}, u32[]{:S(2)}) collective-permute-start(f32[3,22,3,256]{3,1,2,0:T(8,128)S(1)} %get-tuple-element.590), channel_id=1, source_target_pairs={{2,0},{4,2},{6,4},{3,1},{5,3},{7,5},{10,8},{12,10},{14,12},{11,9},... | collective-permute-start | bytes 608264 | tf_op jit(solution)/shard_map/ppermute | solution.py:23
  32.9 8.7 %collective-permute-start.2 = (f32[3,22,3,256]{3,1,2,0:T(8,128)S(1)}, f32[3,22,3,256]{3,1,2,0:T(8,128)S(1)}, u32[]{:S(2)}, u32[]{:S(2)}) collective-permute-start(f32[3,22,3,256]{3,1,2,0:T(8,128)S(1)} %get-tuple-element.589), channel_id=1, source_target_pairs={{0,2},{2,4},{4,6},{1,3},{3,5},{5,7},{8,10},{10,12},{12,14},{9,11},... | collective-permute-start | bytes 608264 | tf_op jit(solution)/shard_map/ppermute | solution.py:21
  46.0 7.8 %collective-permute-start.5 = (f32[3,22,22,3]{2,1,3,0:T(8,128)S(1)}, f32[3,22,22,3]{2,1,3,0:T(8,128)S(1)}, u32[]{:S(2)}, u32[]{:S(2)}) collective-permute-start(f32[3,22,22,3]{2,1,3,0:T(8,128)S(1)} %copy.270), channel_id=1, source_target_pairs={{1,0},{3,2},{5,4},{7,6},{9,8},{11,10},{13,12},{15,14},{17,16},{19,... | collective-permute-start | bytes 52280 | tf_op jit(solution)/shard_map/ppermute | solution.py:23
  49.0 5.5 %collective-permute-start.4 = (f32[3,22,22,3]{2,1,3,0:T(8,128)S(1)}, f32[3,22,22,3]{2,1,3,0:T(8,128)}, u32[]{:S(2)}, u32[]{:S(2)}) collective-permute-start(f32[3,22,22,3]{2,1,3,0:T(8,128)S(1)} %copy.269), channel_id=1, source_target_pairs={{0,1},{2,3},{4,5},{6,7},{8,9},{10,11},{12,13},{14,15},{16,17},{18,... | collective-permute-start | bytes 52280 | tf_op jit(solution)/shard_map/ppermute | solution.py:21
  60.6 36.3 %copy-start.51 = (s32[16,256]{1,0:T(8,128)S(1)}, s32[16,256]{1,0:T(8,128)}, u32[]{:S(2)}) copy-start(s32[16,256]{1,0:T(8,128)} %copy-done.50) | copy-start | bytes 49156
  63.1 35.4 %copy-start.13 = (f32[3,256,256]{1,2,0:T(8,128)S(1)}, f32[3,256,256]{1,2,0:T(8,128)}, u32[]{:S(2)}) copy-start(f32[3,256,256]{1,2,0:T(8,128)} %fusion.132) | copy-start | bytes 2359300
  63.1 35.4 %copy-start.66 = (s32[16]{0:T(128)S(1)}, s32[16]{0:T(128)}, u32[]{:S(2)}) copy-start(s32[16]{0:T(128)} %get-tuple-element.642) | copy-start | bytes 196
  99.1 8.9 %copy-start.6 = (f32[3,256,256]{1,2,0:T(8,128)}, f32[3,256,256]{1,2,0:T(8,128)S(1)}, u32[]{:S(2)}) copy-start(f32[3,256,256]{1,2,0:T(8,128)S(1)} %fusion.77) | copy-start | bytes 2359300
  99.3 14.6 %copy-start.54 = (s32[16,256]{1,0:T(8,128)S(1)}, s32[16,256]{1,0:T(8,128)}, u32[]{:S(2)}) copy-start(s32[16,256]{1,0:T(8,128)} %copy-done.53) | copy-start | bytes 49156
  99.3 7.0 %collective-permute-start.7 = (f32[3,3,16,256]{3,2,1,0:T(8,128)S(1)}, f32[3,3,16,256]{3,2,1,0:T(8,128)S(1)}, u32[]{:S(2)}, u32[]{:S(2)}) collective-permute-start(f32[3,3,16,256]{3,2,1,0:T(8,128)S(1)} %get-tuple-element.614), channel_id=1, source_target_pairs={{8,0},{16,8},{24,16},{9,1},{17,9},{25,17},{10,2},{18,10},{26,18},{... | collective-permute-start | bytes 442376 | tf_op jit(solution)/shard_map/ppermute | solution.py:23
  100.6 7.2 %collective-permute-start.6 = (f32[3,3,16,256]{3,2,1,0:T(8,128)S(1)}, f32[3,3,16,256]{3,2,1,0:T(8,128)S(1)}, u32[]{:S(2)}, u32[]{:S(2)}) collective-permute-start(f32[3,3,16,256]{3,2,1,0:T(8,128)S(1)} %get-tuple-element.613), channel_id=1, source_target_pairs={{0,8},{8,16},{16,24},{1,9},{9,17},{17,25},{2,10},{10,18},{18,26},{... | collective-permute-start | bytes 442376 | tf_op jit(solution)/shard_map/ppermute | solution.py:21
  107.8 9.9 %copy-start.22 = (f32[3,3,16,256]{3,2,1,0:T(8,128)}, f32[3,3,16,256]{3,2,1,0:T(8,128)S(1)}, u32[]{:S(2)}) copy-start(f32[3,3,16,256]{3,2,1,0:T(8,128)S(1)} %collective-permute-done.6) | copy-start | bytes 442372
  108.0 8.1 %collective-permute-start.9 = (f32[3,22,3,256]{3,1,2,0:T(8,128)S(1)}, f32[3,22,3,256]{3,1,2,0:T(8,128)S(1)}, u32[]{:S(2)}, u32[]{:S(2)}) collective-permute-start(f32[3,22,3,256]{3,1,2,0:T(8,128)S(1)} %copy.294), channel_id=1, source_target_pairs={{2,0},{4,2},{6,4},{3,1},{5,3},{7,5},{10,8},{12,10},{14,12},{11,9},... | collective-permute-start | bytes 608264 | tf_op jit(solution)/shard_map/ppermute | solution.py:23
  109.3 8.0 %collective-permute-start.8 = (f32[3,22,3,256]{3,1,2,0:T(8,128)S(1)}, f32[3,22,3,256]{3,1,2,0:T(8,128)S(1)}, u32[]{:S(2)}, u32[]{:S(2)}) collective-permute-start(f32[3,22,3,256]{3,1,2,0:T(8,128)S(1)} %copy.293), channel_id=1, source_target_pairs={{0,2},{2,4},{4,6},{1,3},{3,5},{5,7},{8,10},{10,12},{12,14},{9,11},... | collective-permute-start | bytes 608264 | tf_op jit(solution)/shard_map/ppermute | solution.py:21
  120.8 10.4 %collective-permute-start.11 = (f32[3,22,22,3]{2,1,3,0:T(8,128)S(1)}, f32[3,22,22,3]{2,1,3,0:T(8,128)S(1)}, u32[]{:S(2)}, u32[]{:S(2)}) collective-permute-start(f32[3,22,22,3]{2,1,3,0:T(8,128)S(1)} %copy.298), channel_id=1, source_target_pairs={{1,0},{3,2},{5,4},{7,6},{9,8},{11,10},{13,12},{15,14},{17,16},{19,... | collective-permute-start | bytes 52280 | tf_op jit(solution)/shard_map/ppermute | solution.py:23
  123.8 8.0 %collective-permute-start.10 = (f32[3,22,22,3]{2,1,3,0:T(8,128)S(1)}, f32[3,22,22,3]{2,1,3,0:T(8,128)}, u32[]{:S(2)}, u32[]{:S(2)}) collective-permute-start(f32[3,22,22,3]{2,1,3,0:T(8,128)S(1)} %copy.297), channel_id=1, source_target_pairs={{0,1},{2,3},{4,5},{6,7},{8,9},{10,11},{12,13},{14,15},{16,17},{18,... | collective-permute-start | bytes 52280 | tf_op jit(solution)/shard_map/ppermute | solution.py:21
  149.1 21.1 %copy-start.47 = (s32[16]{0:T(128)S(1)}, s32[16]{0:T(128)}, u32[]{:S(2)}) copy-start(s32[16]{0:T(128)} %copy-done.46) | copy-start | bytes 196
  151.6 32.9 %copy-start.67 = (s32[16]{0:T(128)S(1)}, s32[16]{0:T(128)}, u32[]{:S(2)}) copy-start(s32[16]{0:T(128)} %get-tuple-element.642) | copy-start | bytes 196
  185.2 8.9 %copy-start.8 = (f32[3,256,256]{1,2,0:T(8,128)}, f32[3,256,256]{1,2,0:T(8,128)S(1)}, u32[]{:S(2)}) copy-start(f32[3,256,256]{1,2,0:T(8,128)S(1)} %fusion.76) | copy-start | bytes 2359300
  185.4 15.0 %copy-start.56 = (s32[16,256]{1,0:T(8,128)S(1)}, s32[16,256]{1,0:T(8,128)}, u32[]{:S(2)}) copy-start(s32[16,256]{1,0:T(8,128)} %copy-done.53) | copy-start | bytes 49156
  185.4 7.0 %collective-permute-start.13 = (f32[3,3,16,256]{3,2,1,0:T(8,128)S(1)}, f32[3,3,16,256]{3,2,1,0:T(8,128)S(1)}, u32[]{:S(2)}, u32[]{:S(2)}) collective-permute-start(f32[3,3,16,256]{3,2,1,0:T(8,128)S(1)} %get-tuple-element.610), channel_id=1, source_target_pairs={{8,0},{16,8},{24,16},{9,1},{17,9},{25,17},{10,2},{18,10},{26,18},{... | collective-permute-start | bytes 442376 | tf_op jit(solution)/shard_map/ppermute | solution.py:23
  186.7 7.2 %collective-permute-start.12 = (f32[3,3,16,256]{3,2,1,0:T(8,128)S(1)}, f32[3,3,16,256]{3,2,1,0:T(8,128)S(1)}, u32[]{:S(2)}, u32[]{:S(2)}) collective-permute-start(f32[3,3,16,256]{3,2,1,0:T(8,128)S(1)} %get-tuple-element.609), channel_id=1, source_target_pairs={{0,8},{8,16},{16,24},{1,9},{9,17},{17,25},{2,10},{10,18},{18,26},{... | collective-permute-start | bytes 442376 | tf_op jit(solution)/shard_map/ppermute | solution.py:21
  192.5 11.1 %copy-start.20 = (f32[3,3,16,256]{3,2,1,0:T(8,128)}, f32[3,3,16,256]{3,2,1,0:T(8,128)S(1)}, u32[]{:S(2)}) copy-start(f32[3,3,16,256]{3,2,1,0:T(8,128)S(1)} %collective-permute-done.13) | copy-start | bytes 442372
  193.9 11.1 %copy-start.23 = (f32[3,3,16,256]{3,2,1,0:T(8,128)}, f32[3,3,16,256]{3,2,1,0:T(8,128)S(1)}, u32[]{:S(2)}) copy-start(f32[3,3,16,256]{3,2,1,0:T(8,128)S(1)} %collective-permute-done.12) | copy-start | bytes 442372
  194.1 9.1 %collective-permute-start.15 = (f32[3,22,3,256]{3,1,2,0:T(8,128)S(1)}, f32[3,22,3,256]{3,1,2,0:T(8,128)S(1)}, u32[]{:S(2)}, u32[]{:S(2)}) collective-permute-start(f32[3,22,3,256]{3,1,2,0:T(8,128)S(1)} %copy.320), channel_id=1, source_target_pairs={{2,0},{4,2},{6,4},{3,1},{5,3},{7,5},{10,8},{12,10},{14,12},{11,9},... | collective-permute-start | bytes 608264 | tf_op jit(solution)/shard_map/ppermute | solution.py:23
  195.4 8.0 %collective-permute-start.14 = (f32[3,22,3,256]{3,1,2,0:T(8,128)S(1)}, f32[3,22,3,256]{3,1,2,0:T(8,128)S(1)}, u32[]{:S(2)}, u32[]{:S(2)}) collective-permute-start(f32[3,22,3,256]{3,1,2,0:T(8,128)S(1)} %copy.319), channel_id=1, source_target_pairs={{0,2},{2,4},{4,6},{1,3},{3,5},{5,7},{8,10},{10,12},{12,14},{9,11},... | collective-permute-start | bytes 608264 | tf_op jit(solution)/shard_map/ppermute | solution.py:21
  207.9 8.5 %collective-permute-start.17 = (f32[3,22,22,3]{2,1,3,0:T(8,128)S(1)}, f32[3,22,22,3]{2,1,3,0:T(8,128)S(1)}, u32[]{:S(2)}, u32[]{:S(2)}) collective-permute-start(f32[3,22,22,3]{2,1,3,0:T(8,128)S(1)} %copy.324), channel_id=1, source_target_pairs={{1,0},{3,2},{5,4},{7,6},{9,8},{11,10},{13,12},{15,14},{17,16},{19,... | collective-permute-start | bytes 52280 | tf_op jit(solution)/shard_map/ppermute | solution.py:23
  209.7 8.0 %collective-permute-start.16 = (f32[3,22,22,3]{2,1,3,0:T(8,128)S(1)}, f32[3,22,22,3]{2,1,3,0:T(8,128)S(1)}, u32[]{:S(2)}, u32[]{:S(2)}) collective-permute-start(f32[3,22,22,3]{2,1,3,0:T(8,128)S(1)} %copy.323), channel_id=1, source_target_pairs={{0,1},{2,3},{4,5},{6,7},{8,9},{10,11},{12,13},{14,15},{16,17},{18,... | collective-permute-start | bytes 52280 | tf_op jit(solution)/shard_map/ppermute | solution.py:21
  235.1 23.0 %copy-start.48 = (s32[16]{0:T(128)S(1)}, s32[16]{0:T(128)}, u32[]{:S(2)}) copy-start(s32[16]{0:T(128)} %copy-done.46) | copy-start | bytes 196
  235.1 35.4 %copy-start.52 = (s32[16,256]{1,0:T(8,128)S(1)}, s32[16,256]{1,0:T(8,128)}, u32[]{:S(2)}) copy-start(s32[16,256]{1,0:T(8,128)} %copy-done.50) | copy-start | bytes 49156
  237.6 34.5 %copy-start.68 = (s32[16]{0:T(128)S(1)}, s32[16]{0:T(128)}, u32[]{:S(2)}) copy-start(s32[16]{0:T(128)} %get-tuple-element.642) | copy-start | bytes 196
  272.7 8.9 %copy-start.10 = (f32[3,256,256]{1,2,0:T(8,128)}, f32[3,256,256]{1,2,0:T(8,128)S(1)}, u32[]{:S(2)}) copy-start(f32[3,256,256]{1,2,0:T(8,128)S(1)} %fusion.75) | copy-start | bytes 2359300
  272.9 7.0 %collective-permute-start.19 = (f32[3,3,16,256]{3,2,1,0:T(8,128)S(1)}, f32[3,3,16,256]{3,2,1,0:T(8,128)S(1)}, u32[]{:S(2)}, u32[]{:S(2)}) collective-permute-start(f32[3,3,16,256]{3,2,1,0:T(8,128)S(1)} %get-tuple-element.606), channel_id=1, source_target_pairs={{8,0},{16,8},{24,16},{9,1},{17,9},{25,17},{10,2},{18,10},{26,18},{... | collective-permute-start | bytes 442376 | tf_op jit(solution)/shard_map/ppermute | solution.py:23
  274.2 7.2 %collective-permute-start.18 = (f32[3,3,16,256]{3,2,1,0:T(8,128)S(1)}, f32[3,3,16,256]{3,2,1,0:T(8,128)S(1)}, u32[]{:S(2)}, u32[]{:S(2)}) collective-permute-start(f32[3,3,16,256]{3,2,1,0:T(8,128)S(1)} %get-tuple-element.605), channel_id=1, source_target_pairs={{0,8},{8,16},{16,24},{1,9},{9,17},{17,25},{2,10},{10,18},{18,26},{... | collective-permute-start | bytes 442376 | tf_op jit(solution)/shard_map/ppermute | solution.py:21
  281.5 9.9 %copy-start.24 = (f32[3,3,16,256]{3,2,1,0:T(8,128)}, f32[3,3,16,256]{3,2,1,0:T(8,128)S(1)}, u32[]{:S(2)}) copy-start(f32[3,3,16,256]{3,2,1,0:T(8,128)S(1)} %collective-permute-done.18) | copy-start | bytes 442372
  281.6 8.1 %collective-permute-start.21 = (f32[3,22,3,256]{3,1,2,0:T(8,128)S(1)}, f32[3,22,3,256]{3,1,2,0:T(8,128)S(1)}, u32[]{:S(2)}, u32[]{:S(2)}) collective-permute-start(f32[3,22,3,256]{3,1,2,0:T(8,128)S(1)} %copy.346), channel_id=1, source_target_pairs={{2,0},{4,2},{6,4},{3,1},{5,3},{7,5},{10,8},{12,10},{14,12},{11,9},... | collective-permute-start | bytes 608264 | tf_op jit(solution)/shard_map/ppermute | solution.py:23
  283.0 8.0 %collective-permute-start.20 = (f32[3,22,3,256]{3,1,2,0:T(8,128)S(1)}, f32[3,22,3,256]{3,1,2,0:T(8,128)S(1)}, u32[]{:S(2)}, u32[]{:S(2)}) collective-permute-start(f32[3,22,3,256]{3,1,2,0:T(8,128)S(1)} %copy.345), channel_id=1, source_target_pairs={{0,2},{2,4},{4,6},{1,3},{3,5},{5,7},{8,10},{10,12},{12,14},{9,11},... | collective-permute-start | bytes 608264 | tf_op jit(solution)/shard_map/ppermute | solution.py:21
  294.5 10.4 %collective-permute-start.23 = (f32[3,22,22,3]{2,1,3,0:T(8,128)S(1)}, f32[3,22,22,3]{2,1,3,0:T(8,128)S(1)}, u32[]{:S(2)}, u32[]{:S(2)}) collective-permute-start(f32[3,22,22,3]{2,1,3,0:T(8,128)S(1)} %copy.350), channel_id=1, source_target_pairs={{1,0},{3,2},{5,4},{7,6},{9,8},{11,10},{13,12},{15,14},{17,16},{19,... | collective-permute-start | bytes 52280 | tf_op jit(solution)/shard_map/ppermute | solution.py:23
  297.4 7.9 %collective-permute-start.22 = (f32[3,22,22,3]{2,1,3,0:T(8,128)S(1)}, f32[3,22,22,3]{2,1,3,0:T(8,128)}, u32[]{:S(2)}, u32[]{:S(2)}) collective-permute-start(f32[3,22,22,3]{2,1,3,0:T(8,128)S(1)} %copy.349), channel_id=1, source_target_pairs={{0,1},{2,3},{4,5},{6,7},{8,9},{10,11},{12,13},{14,15},{16,17},{18,... | collective-permute-start | bytes 52280 | tf_op jit(solution)/shard_map/ppermute | solution.py:21
  325.3 32.7 %copy-start.69 = (s32[16]{0:T(128)S(1)}, s32[16]{0:T(128)}, u32[]{:S(2)}) copy-start(s32[16]{0:T(128)} %get-tuple-element.642) | copy-start | bytes 196
  358.6 8.9 %copy-start.12 = (f32[3,256,256]{1,2,0:T(8,128)}, f32[3,256,256]{1,2,0:T(8,128)S(1)}, u32[]{:S(2)}) copy-start(f32[3,256,256]{1,2,0:T(8,128)S(1)} %fusion.74) | copy-start | bytes 2359300
  358.8 14.8 %copy-start.59 = (s32[16,256]{1,0:T(8,128)S(1)}, s32[16,256]{1,0:T(8,128)}, u32[]{:S(2)}) copy-start(s32[16,256]{1,0:T(8,128)} %copy-done.53) | copy-start | bytes 49156
  358.9 7.0 %collective-permute-start.25 = (f32[3,3,16,256]{3,2,1,0:T(8,128)S(1)}, f32[3,3,16,256]{3,2,1,0:T(8,128)S(1)}, u32[]{:S(2)}, u32[]{:S(2)}) collective-permute-start(f32[3,3,16,256]{3,2,1,0:T(8,128)S(1)} %get-tuple-element.602), channel_id=1, source_target_pairs={{8,0},{16,8},{24,16},{9,1},{17,9},{25,17},{10,2},{18,10},{26,18},{... | collective-permute-start | bytes 442376 | tf_op jit(solution)/shard_map/ppermute | solution.py:23
  360.2 7.2 %collective-permute-start.24 = (f32[3,3,16,256]{3,2,1,0:T(8,128)S(1)}, f32[3,3,16,256]{3,2,1,0:T(8,128)S(1)}, u32[]{:S(2)}, u32[]{:S(2)}) collective-permute-start(f32[3,3,16,256]{3,2,1,0:T(8,128)S(1)} %get-tuple-element.601), channel_id=1, source_target_pairs={{0,8},{8,16},{16,24},{1,9},{9,17},{17,25},{2,10},{10,18},{18,26},{... | collective-permute-start | bytes 442376 | tf_op jit(solution)/shard_map/ppermute | solution.py:21
  365.9 11.1 %copy-start.21 = (f32[3,3,16,256]{3,2,1,0:T(8,128)}, f32[3,3,16,256]{3,2,1,0:T(8,128)S(1)}, u32[]{:S(2)}) copy-start(f32[3,3,16,256]{3,2,1,0:T(8,128)S(1)} %collective-permute-done.25) | copy-start | bytes 442372
  367.4 10.9 %copy-start.25 = (f32[3,3,16,256]{3,2,1,0:T(8,128)}, f32[3,3,16,256]{3,2,1,0:T(8,128)S(1)}, u32[]{:S(2)}) copy-start(f32[3,3,16,256]{3,2,1,0:T(8,128)S(1)} %collective-permute-done.24) | copy-start | bytes 442372
  367.5 8.9 %collective-permute-start.27 = (f32[3,22,3,256]{3,1,2,0:T(8,128)S(1)}, f32[3,22,3,256]{3,1,2,0:T(8,128)S(1)}, u32[]{:S(2)}, u32[]{:S(2)}) collective-permute-start(f32[3,22,3,256]{3,1,2,0:T(8,128)S(1)} %copy.372), channel_id=1, source_target_pairs={{2,0},{4,2},{6,4},{3,1},{5,3},{7,5},{10,8},{12,10},{14,12},{11,9},... | collective-permute-start | bytes 608264 | tf_op jit(solution)/shard_map/ppermute | solution.py:23
  368.9 8.0 %collective-permute-start.26 = (f32[3,22,3,256]{3,1,2,0:T(8,128)S(1)}, f32[3,22,3,256]{3,1,2,0:T(8,128)S(1)}, u32[]{:S(2)}, u32[]{:S(2)}) collective-permute-start(f32[3,22,3,256]{3,1,2,0:T(8,128)S(1)} %copy.371), channel_id=1, source_target_pairs={{0,2},{2,4},{4,6},{1,3},{3,5},{5,7},{8,10},{10,12},{12,14},{9,11},... | collective-permute-start | bytes 608264 | tf_op jit(solution)/shard_map/ppermute | solution.py:21
  381.1 8.5 %collective-permute-start.29 = (f32[3,22,22,3]{2,1,3,0:T(8,128)S(1)}, f32[3,22,22,3]{2,1,3,0:T(8,128)S(1)}, u32[]{:S(2)}, u32[]{:S(2)}) collective-permute-start(f32[3,22,22,3]{2,1,3,0:T(8,128)S(1)} %copy.376), channel_id=1, source_target_pairs={{1,0},{3,2},{5,4},{7,6},{9,8},{11,10},{13,12},{15,14},{17,16},{19,... | collective-permute-start | bytes 52280 | tf_op jit(solution)/shard_map/ppermute | solution.py:23
  383.0 8.0 %collective-permute-start.28 = (f32[3,22,22,3]{2,1,3,0:T(8,128)S(1)}, f32[3,22,22,3]{2,1,3,0:T(8,128)S(1)}, u32[]{:S(2)}, u32[]{:S(2)}) collective-permute-start(f32[3,22,22,3]{2,1,3,0:T(8,128)S(1)} %copy.375), channel_id=1, source_target_pairs={{0,1},{2,3},{4,5},{6,7},{8,9},{10,11},{12,13},{14,15},{16,17},{18,... | collective-permute-start | bytes 52280 | tf_op jit(solution)/shard_map/ppermute | solution.py:21
  410.7 37.1 %copy-start.7 = (f32[3,256,256]{1,2,0:T(8,128)S(1)}, f32[3,256,256]{1,2,0:T(8,128)}, u32[]{:S(2)}) copy-start(f32[3,256,256]{1,2,0:T(8,128)} %copy-done.6) | copy-start | bytes 2359300
  410.7 37.2 %copy-start.9 = (f32[3,256,256]{1,2,0:T(8,128)S(1)}, f32[3,256,256]{1,2,0:T(8,128)}, u32[]{:S(2)}) copy-start(f32[3,256,256]{1,2,0:T(8,128)} %copy-done.8) | copy-start | bytes 2359300
  410.7 37.2 %copy-start.11 = (f32[3,256,256]{1,2,0:T(8,128)S(1)}, f32[3,256,256]{1,2,0:T(8,128)}, u32[]{:S(2)}) copy-start(f32[3,256,256]{1,2,0:T(8,128)} %copy-done.10) | copy-start | bytes 2359300
  (37 other events, 166.1 us)
